TPU v7x, 32 devices: a whole 2x2x4 slice. The times are simulated.
32 devices in a mesh: tp: 8 (over z, y), dp: 4 (over x, core).
Axes of the slice: x: 2, y: 2, z: 4, core: 2. Of those that a mesh axis runs over, the one named last changes fastest.
Arguments:
- tokens: bfloat16 [768, 4096], P(('dp', 'tp')), may hold values from -6 to 6
- hidden_grad: bfloat16 [768, 14336], P('dp', 'tp'), may hold values from -0.59765625 to 0.59765625
- gate_value: bfloat16 [768, 14336], P('dp', 'tp'), may hold values from -6 to 6
- up_value: bfloat16 [768, 14336], P('dp', 'tp'), may hold values from -6 to 6
- gate_weight: bfloat16 [4096, 14336], P('dp', 'tp'), may hold values from -0.09375 to 0.09375
- up_weight: bfloat16 [4096, 14336], P('dp', 'tp'), may hold values from -0.09375 to 0.09375
Outputs:
- input_grad: bfloat16 [768, 4096], P(('dp', 'tp'))
- gate_grad: bfloat16 [4096, 14336], P('dp', 'tp')
- up_grad: bfloat16 [4096, 14336], P('dp', 'tp')
All inputs are finite; a program needn't handle non-finite values.
Results may differ from a plain program's by a relative error of at most 0.018.
Values may be sent and summed in bfloat16 or wider, within the bound.
A program may use at most 128 MiB of HBM per device.

v0:
```python
import jax
import jax.numpy as jnp
from jax import lax
from jax.sharding import PartitionSpec as P


def on_device(tokens, hidden_grad, gate_value, up_value, gate_weight, up_weight):
    n_dp = lax.axis_size("dp")
    n_tp = lax.axis_size("tp")
    token_rows, features = tokens.shape
    width = gate_weight.shape[0]
    hidden_width = gate_value.shape[1]
    gate_float = gate_value.astype(jnp.float32)
    up_float = up_value.astype(jnp.float32)
    logistic = jax.nn.sigmoid(gate_float)
    upstream = hidden_grad.astype(jnp.float32)
    d_gate = (upstream * up_float * logistic * (1.0 + gate_float * (1.0 - logistic))).astype(
        jnp.bfloat16
    )
    d_up = (upstream * gate_float * logistic).astype(jnp.bfloat16)
    pieces = lax.all_gather(jnp.concatenate([d_gate, d_up], axis=1), "dp", axis=0, tiled=True)
    mine = lax.all_to_all(tokens, "dp", split_axis=1, concat_axis=0, tiled=True)
    columns = lax.all_gather(mine, "tp", axis=0, tiled=True)
    columns = columns.reshape(n_tp, n_dp, token_rows, width).transpose(1, 0, 2, 3)
    columns = columns.reshape(n_tp * n_dp * token_rows, width)
    across = (((1,), (1,)), ((), ()))
    contract = (((0,), (0,)), ((), ()))
    partial = (
        lax.dot_general(
            pieces[:, :hidden_width], gate_weight, across, preferred_element_type=jnp.float32
        )
        + lax.dot_general(
            pieces[:, hidden_width:], up_weight, across, preferred_element_type=jnp.float32
        )
    ).astype(jnp.bfloat16)
    partial = partial.reshape(n_dp, n_tp, token_rows, width).transpose(1, 0, 2, 3)
    partial = partial.reshape(n_tp * n_dp * token_rows, width)
    summed = lax.psum_scatter(partial, "tp", scatter_dimension=0, tiled=True)
    input_grad = lax.all_to_all(summed, "dp", split_axis=0, concat_axis=1, tiled=True)
    gate_grad = lax.dot_general(
        columns, pieces[:, :hidden_width], contract, preferred_element_type=jnp.float32
    ).astype(jnp.bfloat16)
    up_grad = lax.dot_general(
        columns, pieces[:, hidden_width:], contract, preferred_element_type=jnp.float32
    ).astype(jnp.bfloat16)
    return (input_grad, gate_grad, up_grad)


def solution(mesh):
    placed = (
        P(("dp", "tp"), None),
        P("dp", "tp"),
        P("dp", "tp"),
        P("dp", "tp"),
        P("dp", "tp"),
        P("dp", "tp"),
    )
    return jax.shard_map(
        on_device,
        mesh=mesh,
        in_specs=placed,
        out_specs=(P(("dp", "tp"), None), P("dp", "tp"), P("dp", "tp")),
        check_vma=False,
    )
```

profile of v0, /device:TPU:0, one launch (start us, length us, event | category | flops | bytes accessed | tf_op | source)
XLA Modules:
  0.0 198.5 jit_solution(8815059297840828324)
XLA Ops:
  7.2 0.0 all-gather.3.cloned.1.call-start
  7.2 2.2 %fusion.12 = (bf16[192,1792]{1,0:T(8,128)(2,1)S(1)}, bf16[192,1792]{1,0:T(8,128)(2,1)S(1)}) fusion(bf16[192,1792]{1,0:T(8,128)(2,1)} %param.7, bf16[192,1792]{1,0:T(8,128)(2,1)} %param.8, bf16[192,1792]{1,0:T(8,128)(2,1)} %param.9), kind=kLoop, calls=%fused_computation.17 | loop fusion | flops 5505024 | bytes 3440640 | tf_op jit(solution)/shard_map/convert_element_type | solution.py:17
  9.4 0.0 copy-start
  9.5 1.2 pad_maximum_fusion
  10.6 0.0 all-gather.3.cloned.1.call-update
  10.6 0.0 all-gather.5.cloned.1.call-start
  10.7 9.4 %all_to_all.38 = bf16[24,4,1024]{2,0,1:T(8,128)(2,1)} all-to-all(bf16[24,4,1024]{2,0,1:T(8,128)(2,1)S(1)} %bitcast.34), channel_id=1, replica_groups=mesh['tp'=8,'dp'=4] {'dp'}, dimensions={1} | all-to-all | bytes 393216 | tf_op jit(solution)/shard_map/all_to_all | solution.py:22
  20.2 0.0 all-gather.5.cloned.1.call-update
  20.2 0.0 reduce-scatter.2.cloned.1.call-start
  20.2 35.2 %all-gather.3.cloned.1.call-done = bf16[768,3584]{1,0:T(8,128)(2,1)} async-done(((bf16[192,3584]{1,0:T(8,128)(2,1)}), bf16[768,3584]{1,0:T(8,128)(2,1)}) %all-gather.3.cloned.1.call-update) | async-done | bytes 5505040 | tf_op jit(solution)/shard_map/all_gather | solution.py:21
  55.4 6.0 %fusion.3 = f32[768,1024]{1,0:T(8,128)S(1)} fusion(bf16[1024,1792]{1,0:T(8,128)(2,1)} %param.11, bf16[768,3584]{1,0:T(8,128)(2,1)} %all-gather.3.cloned.1.call-done), kind=kOutput, calls=%fused_computation.6 | convolution fusion | flops 2818572288 | bytes 9568256 | tf_op jit(solution)/shard_map/dot_general | solution.py:32
  61.5 3.0 %add_convert_fusion = bf16[768,1024]{1,0:T(8,128)(2,1)S(1)} fusion(f32[768,1024]{1,0:T(8,128)S(1)} %fusion.3, bf16[1024,1792]{1,0:T(8,128)(2,1)S(1)} %copy-done.2, bf16[768,3584]{1,0:T(8,128)(2,1)S(1)} %copy-done.1), kind=kOutput, calls=%fused_computation.4 | convolution fusion | flops 2820145152 | bytes 11141120 | tf_op jit(solution)/shard_map/dot_general | solution.py:29
  64.5 1.3 copy.21
  65.8 0.0 reduce-scatter.2.cloned.1.call-update
  65.8 36.0 %all-gather.5.cloned.1.call-done = bf16[768,1024]{1,0:T(8,128)(2,1)} async-done(((bf16[96,1024]{1,0:T(8,128)(2,1)}), bf16[768,1024]{1,0:T(8,128)(2,1)}) %all-gather.5.cloned.1.call-update) | async-done | bytes 1572880 | tf_op jit(solution)/shard_map/all_gather | solution.py:23
  101.8 1.6 copy.24
  103.4 6.4 %fusion = bf16[1024,1792]{0,1:T(8,128)(2,1)} fusion(bf16[768,1024]{1,0:T(8,128)(2,1)S(1)} %bitcast.29, bf16[768,3584]{1,0:T(8,128)(2,1)} %all-gather.3.cloned.1.call-done), kind=kOutput, calls=%fused_computation.2 | convolution fusion | flops 2820407296 | bytes 7995392 | tf_op jit(solution)/shard_map/dot_general | solution.py:40
  109.8 60.0 %reduce-scatter.2.cloned.1.call-done = bf16[96,1024]{1,0:T(8,128)(2,1)} async-done(((bf16[768,1024]{1,0:T(8,128)(2,1)}), bf16[96,1024]{1,0:T(8,128)(2,1)}) %reduce-scatter.2.cloned.1.call-update) | async-done | bytes 196624 | tf_op jit(solution)/shard_map/reduce_scatter | solution.py:38
  169.8 3.4 %all-to-all-start = ((bf16[4,24,1024]{2,1,0:T(8,128)(2,1)}), bf16[4,24,1024]{2,1,0:T(8,128)(2,1)S(1)}, u32[]{:S(2)}, u32[]{:S(2)}) async-start(bf16[4,24,1024]{2,1,0:T(8,128)(2,1)} %bitcast.36), calls=%async_computation.1 | async-start | bytes 393216 | tf_op jit(solution)/shard_map/all_to_all | solution.py:39
  173.1 6.3 %fusion.1 = bf16[1024,1792]{0,1:T(8,128)(2,1)} fusion(bf16[768,1024]{1,0:T(8,128)(2,1)S(1)} %bitcast.30, bf16[768,3584]{1,0:T(8,128)(2,1)} %all-gather.3.cloned.1.call-done), kind=kOutput, calls=%fused_computation.3 | convolution fusion | flops 2820407296 | bytes 7995392 | tf_op jit(solution)/shard_map/dot_general | solution.py:43
  179.4 5.9 %copy.26 = bf16[1024,1792]{1,0:T(8,128)(2,1)} copy(bf16[1024,1792]{0,1:T(8,128)(2,1)} %fusion.1) | data formatting | bytes 7340032
  185.3 5.9 %copy.25 = bf16[1024,1792]{1,0:T(8,128)(2,1)} copy(bf16[1024,1792]{0,1:T(8,128)(2,1)} %fusion) | data formatting | bytes 7340032
  191.3 0.0 all-to-all-done
  191.3 0.7 copy.28
  (6 shorter events, 0.0 us)
Async XLA Ops:
  7.2 48.3 %all-gather.3.cloned.1.call-start = ((), (), s32[]{:S(2)}) async-start(), calls=%async_computation.3 | async-start | bytes 6881280 | tf_op jit(solution)/shard_map/all_gather | solution.py:21
  9.4 1.3 copy-start
  10.6 91.2 %all-gather.5.cloned.1.call-start = ((), (), s32[]{:S(2)}) async-start(), calls=%async_computation.5 | async-start | bytes 1769472 | tf_op jit(solution)/shard_map/all_gather | solution.py:23
  20.2 149.6 %reduce-scatter.2.cloned.1.call-start = ((), (), s32[]{:S(2)}) async-start(), calls=%async_computation.4 | async-start | bytes 1769472 | tf_op jit(solution)/shard_map/reduce_scatter | solution.py:38
  55.4 6.1 %copy-start.1 = (bf16[768,3584]{1,0:T(8,128)(2,1)S(1)}, bf16[768,3584]{1,0:T(8,128)(2,1)}, u32[]{:S(2)}) copy-start(bf16[768,3584]{1,0:T(8,128)(2,1)} %all-gather.3.cloned.1.call-done) | copy-start | bytes 16515076
  55.4 6.1 %copy-start.2 = (bf16[1024,1792]{1,0:T(8,128)(2,1)S(1)}, bf16[1024,1792]{1,0:T(8,128)(2,1)}, u32[]{:S(2)}) copy-start(bf16[1024,1792]{1,0:T(8,128)(2,1)} %param.10) | copy-start | bytes 11010052
  169.8 21.5 %all-to-all-start = ((bf16[4,24,1024]{2,1,0:T(8,128)(2,1)}), bf16[4,24,1024]{2,1,0:T(8,128)(2,1)S(1)}, u32[]{:S(2)}, u32[]{:S(2)}) async-start(bf16[4,24,1024]{2,1,0:T(8,128)(2,1)} %bitcast.36), calls=%async_computation.1 | async-start | bytes 393216 | tf_op jit(solution)/shard_map/all_to_all | solution.py:39
Sparse Core Ops, SparseCore 0:
  10.8 44.6 all-gather.2
  57.6 44.1 all-gather.4
  105.8 63.8 reduce-scatter.1
where the time goes:
time: 199 us; the launch traced here: 198 us
  waiting for transfers between devices  131 us (66%)
  matrix products  21.8 us (11%)
  local copies, waits for them, and re-layouts  15.4 us (8%)
  between operations  13.8 us (7%)
  blocking collectives  9.44 us (5%)
  starting transfers between devices  3.49 us (2%)
  other arithmetic  3.4 us (2%)
    reduce_scatter x1, waiting for transfers between devices, on_device(): summed = lax.psum_scatter(partial, 'tp', scatter_dimension=0, tiled=True)  60 us
    all_gather x1, waiting for transfers between devices, on_device(): columns = lax.all_gather(mine, 'tp', axis=0, tiled=True)  36 us
    all_gather x1, waiting for transfers between devices, on_device(): lax.all_gather(jnp.concatenate([d_gate, d_up], axis=1), 'dp', axis=0, til...  35.2 us
    unnamed x8, local copies, waits for them, and re-layouts  11.8 us
    all_to_all x1, blocking collectives, on_device(): mine = lax.all_to_all(tokens, 'dp', split_axis=1, concat_axis=0, tiled=True)  9.44 us
    dot_general x1, matrix products, on_device(): lax.dot_general(columns, pieces[:, :hidden_width], contract, preferred_el...  6.42 us
    dot_general x1, matrix products, on_device(): lax.dot_general(columns, pieces[:, hidden_width:], contract, preferred_el...  6.3 us
    dot_general x1, matrix products, on_device(): lax.dot_general(pieces[:, hidden_width:], up_weight, across, preferred_el...  6.04 us
  transfers between devices with their start and end apart: 4, of which 3 were waited for; matrix products, arithmetic and copies ran while one was open for 18% of the time, Pallas kernels for 0%

commit v1 on v0

--- a/solution.py
+++ b/solution.py
@@ -20,7 +20,9 @@
     d_up = (upstream * gate_float * logistic).astype(jnp.bfloat16)
     pieces = lax.all_gather(jnp.concatenate([d_gate, d_up], axis=1), "dp", axis=0, tiled=True)
     mine = lax.all_to_all(tokens, "dp", split_axis=1, concat_axis=0, tiled=True)
-    columns = lax.all_gather(mine, "tp", axis=0, tiled=True)
+    columns = jnp.concatenate(
+        lax.all_to_all(jnp.stack([mine] * lax.axis_size("tp")), "tp", 0, 0), axis=0
+    )
     columns = columns.reshape(n_tp, n_dp, token_rows, width).transpose(1, 0, 2, 3)
     columns = columns.reshape(n_tp * n_dp * token_rows, width)
     across = (((1,), (1,)), ((), ()))

time: 199 us -> 161 us (0.81)
  waiting for transfers between devices: 131 us -> 87.3 us
  starting transfers between devices: 3.49 us -> 9.27 us
    all_gather x1 -> x0, waiting for transfers between devices: 36 us -> none  [on_device(): columns = lax.all_gather(mine, 'tp', axis=0, tiled=True)]
    all_gather x1, waiting for transfers between devices: 35.2 us -> 28.2 us  [on_device(): lax.all_gather(jnp.concatenate([d_gate, d_up], axis=1), 'dp', axis=0, til...]
    all_to_all x0 -> x1, starting transfers between devices: none -> 5.83 us  [on_device(): lax.all_to_all(jnp.stack([mine] * lax.axis_size('tp')), 'tp', 0, 0)]
  transfers between devices with their start and end apart: 4 -> 4, of which waited for: 3 -> 2; matrix products, arithmetic and copies ran while one was open for 18% -> 23% of each run, Pallas kernels for 0% -> 0%
where the time goes in v1:
time: 161 us
  waiting for transfers between devices  87.3 us (54%)
  matrix products  21.8 us (14%)
  local copies, waits for them, and re-layouts  15.3 us (10%)
  between operations  14.1 us (9%)
  blocking collectives  9.34 us (6%)
  starting transfers between devices  9.27 us (6%)
  other arithmetic  3.4 us (2%)
    reduce_scatter x1, waiting for transfers between devices, on_device(): summed = lax.psum_scatter(partial, 'tp', scatter_dimension=0, tiled=True)  59.1 us
    all_gather x1, waiting for transfers between devices, on_device(): lax.all_gather(jnp.concatenate([d_gate, d_up], axis=1), 'dp', axis=0, til...  28.2 us
    unnamed x8, local copies, waits for them, and re-layouts  11.8 us
    all_to_all x1, blocking collectives, on_device(): mine = lax.all_to_all(tokens, 'dp', split_axis=1, concat_axis=0, tiled=True)  9.34 us
    dot_general x1, matrix products, on_device(): lax.dot_general(columns, pieces[:, :hidden_width], contract, preferred_el...  6.42 us
    dot_general x1, matrix products, on_device(): lax.dot_general(columns, pieces[:, hidden_width:], contract, preferred_el...  6.3 us
    dot_general x1, matrix products, on_device(): lax.dot_general(pieces[:, hidden_width:], up_weight, across, preferred_el...  6.04 us
    all_to_all x1, starting transfers between devices, on_device(): lax.all_to_all(jnp.stack([mine] * lax.axis_size('tp')), 'tp', 0, 0)  5.83 us
  transfers between devices with their start and end apart: 4, of which 2 were waited for; matrix products, arithmetic and copies ran while one was open for 23% of the time, Pallas kernels for 0%

profile of v1, /device:TPU:0, one launch (start us, length us, event | category | flops | bytes accessed | tf_op | source)
XLA Modules:
  0.0 160.6 jit_solution(6959744360783251849)
XLA Ops:
  7.2 0.0 all-gather.2.cloned.1.call-start
  7.2 2.2 %fusion.12 = (bf16[192,1792]{1,0:T(8,128)(2,1)S(1)}, bf16[192,1792]{1,0:T(8,128)(2,1)S(1)}) fusion(bf16[192,1792]{1,0:T(8,128)(2,1)} %param.7, bf16[192,1792]{1,0:T(8,128)(2,1)} %param.8, bf16[192,1792]{1,0:T(8,128)(2,1)} %param.9), kind=kLoop, calls=%fused_computation.17 | loop fusion | flops 5505024 | bytes 3440640 | tf_op jit(solution)/shard_map/convert_element_type | solution.py:17
  9.4 0.0 copy-start
  9.5 1.2 pad_maximum_fusion
  10.6 0.0 all-gather.2.cloned.1.call-update
  10.7 9.3 %all_to_all.40 = bf16[24,4,1024]{2,0,1:T(8,128)(2,1)S(1)} all-to-all(bf16[24,4,1024]{2,0,1:T(8,128)(2,1)S(1)} %bitcast.34), channel_id=1, replica_groups=mesh['tp'=8,'dp'=4] {'dp'}, dimensions={1} | all-to-all | bytes 393216 | tf_op jit(solution)/shard_map/all_to_all | solution.py:22
  20.0 1.3 stack.5
  21.4 5.8 %all-to-all-start.2 = ((bf16[8,96,1024]{2,1,0:T(8,128)(2,1)}), bf16[8,96,1024]{2,1,0:T(8,128)(2,1)S(1)}, u32[]{:S(2)}, u32[]{:S(2)}) async-start(bf16[8,96,1024]{2,1,0:T(8,128)(2,1)} %stack.5), calls=%async_computation.3 | async-start | bytes 3145728 | tf_op jit(solution)/shard_map/all_to_all | solution.py:24
  27.2 0.0 reduce-scatter.2.cloned.1.call-start
  27.2 28.2 %all-gather.2.cloned.1.call-done = bf16[768,3584]{1,0:T(8,128)(2,1)} async-done(((bf16[192,3584]{1,0:T(8,128)(2,1)}), bf16[768,3584]{1,0:T(8,128)(2,1)}) %all-gather.2.cloned.1.call-update) | async-done | bytes 5505040 | tf_op jit(solution)/shard_map/all_gather | solution.py:21
  55.4 6.0 %fusion.3 = f32[768,1024]{1,0:T(8,128)S(1)} fusion(bf16[1024,1792]{1,0:T(8,128)(2,1)} %param.11, bf16[768,3584]{1,0:T(8,128)(2,1)} %all-gather.2.cloned.1.call-done), kind=kOutput, calls=%fused_computation.6 | convolution fusion | flops 2818572288 | bytes 9568256 | tf_op jit(solution)/shard_map/dot_general | solution.py:34
  61.5 3.0 %add_convert_fusion = bf16[768,1024]{1,0:T(8,128)(2,1)S(1)} fusion(f32[768,1024]{1,0:T(8,128)S(1)} %fusion.3, bf16[1024,1792]{1,0:T(8,128)(2,1)S(1)} %copy-done.2, bf16[768,3584]{1,0:T(8,128)(2,1)S(1)} %copy-done.1), kind=kOutput, calls=%fused_computation.4 | convolution fusion | flops 2820145152 | bytes 11141120 | tf_op jit(solution)/shard_map/dot_general | solution.py:31
  64.5 1.3 copy.20
  65.8 0.0 reduce-scatter.2.cloned.1.call-update
  65.8 0.0 all-to-all-done.2
  65.8 0.2 copy.23
  66.0 6.4 %fusion = bf16[1024,1792]{0,1:T(8,128)(2,1)} fusion(bf16[768,1024]{1,0:T(8,128)(2,1)S(1)} %bitcast.29, bf16[768,3584]{1,0:T(8,128)(2,1)} %all-gather.2.cloned.1.call-done), kind=kOutput, calls=%fused_computation.2 | convolution fusion | flops 2820407296 | bytes 7995392 | tf_op jit(solution)/shard_map/dot_general | solution.py:42
  72.4 59.1 %reduce-scatter.2.cloned.1.call-done = bf16[96,1024]{1,0:T(8,128)(2,1)} async-done(((bf16[768,1024]{1,0:T(8,128)(2,1)}), bf16[96,1024]{1,0:T(8,128)(2,1)}) %reduce-scatter.2.cloned.1.call-update) | async-done | bytes 196624 | tf_op jit(solution)/shard_map/reduce_scatter | solution.py:40
  131.5 3.4 %all-to-all-start = ((bf16[4,24,1024]{2,1,0:T(8,128)(2,1)}), bf16[4,24,1024]{2,1,0:T(8,128)(2,1)S(1)}, u32[]{:S(2)}, u32[]{:S(2)}) async-start(bf16[4,24,1024]{2,1,0:T(8,128)(2,1)} %bitcast.36), calls=%async_computation.1 | async-start | bytes 393216 | tf_op jit(solution)/shard_map/all_to_all | solution.py:41
  134.9 6.3 %fusion.1 = bf16[1024,1792]{0,1:T(8,128)(2,1)} fusion(bf16[768,1024]{1,0:T(8,128)(2,1)S(1)} %bitcast.30, bf16[768,3584]{1,0:T(8,128)(2,1)} %all-gather.2.cloned.1.call-done), kind=kOutput, calls=%fused_computation.3 | convolution fusion | flops 2820407296 | bytes 7995392 | tf_op jit(solution)/shard_map/dot_general | solution.py:45
  141.2 5.9 %copy.25 = bf16[1024,1792]{1,0:T(8,128)(2,1)} copy(bf16[1024,1792]{0,1:T(8,128)(2,1)} %fusion.1) | data formatting | bytes 7340032
  147.1 5.9 %copy.24 = bf16[1024,1792]{1,0:T(8,128)(2,1)} copy(bf16[1024,1792]{0,1:T(8,128)(2,1)} %fusion) | data formatting | bytes 7340032
  153.0 0.0 all-to-all-done
  153.0 0.7 copy.27
  (6 shorter events, 0.0 us)
Async XLA Ops:
  7.2 48.3 %all-gather.2.cloned.1.call-start = ((), (), s32[]{:S(2)}) async-start(), calls=%async_computation.4 | async-start | bytes 6881280 | tf_op jit(solution)/shard_map/all_gather | solution.py:21
  9.4 1.2 copy-start
  21.4 44.5 %all-to-all-start.2 = ((bf16[8,96,1024]{2,1,0:T(8,128)(2,1)}), bf16[8,96,1024]{2,1,0:T(8,128)(2,1)S(1)}, u32[]{:S(2)}, u32[]{:S(2)}) async-start(bf16[8,96,1024]{2,1,0:T(8,128)(2,1)} %stack.5), calls=%async_computation.3 | async-start | bytes 3145728 | tf_op jit(solution)/shard_map/all_to_all | solution.py:24
  27.2 104.3 %reduce-scatter.2.cloned.1.call-start = ((), (), s32[]{:S(2)}) async-start(), calls=%async_computation.5 | async-start | bytes 1769472 | tf_op jit(solution)/shard_map/reduce_scatter | solution.py:40
  55.4 6.1 %copy-start.1 = (bf16[768,3584]{1,0:T(8,128)(2,1)S(1)}, bf16[768,3584]{1,0:T(8,128)(2,1)}, u32[]{:S(2)}) copy-start(bf16[768,3584]{1,0:T(8,128)(2,1)} %all-gather.2.cloned.1.call-done) | copy-start | bytes 16515076
  55.4 6.1 %copy-start.2 = (bf16[1024,1792]{1,0:T(8,128)(2,1)S(1)}, bf16[1024,1792]{1,0:T(8,128)(2,1)}, u32[]{:S(2)}) copy-start(bf16[1024,1792]{1,0:T(8,128)(2,1)} %param.10) | copy-start | bytes 11010052
  131.5 21.5 %all-to-all-start = ((bf16[4,24,1024]{2,1,0:T(8,128)(2,1)}), bf16[4,24,1024]{2,1,0:T(8,128)(2,1)S(1)}, u32[]{:S(2)}, u32[]{:S(2)}) async-start(bf16[4,24,1024]{2,1,0:T(8,128)(2,1)} %bitcast.36), calls=%async_computation.1 | async-start | bytes 393216 | tf_op jit(solution)/shard_map/all_to_all | solution.py:41
Sparse Core Ops, SparseCore 0:
  10.8 44.6 all-gather.1
  65.9 65.5 reduce-scatter.1
